TPU v7x, 32 devices: a whole 2x2x4 slice. The times are simulated.
32 devices in a mesh: section: 2 (over core), fsdp: 4 (over z), replica: 4 (over y, x).
Axes of the slice: x: 2, y: 2, z: 4, core: 2. Of those that a mesh axis runs over, the one named last changes fastest.
Arguments:
- tokens_in: bfloat16 [2048, 2048], P(('fsdp', 'replica')), may hold values from -6 to 6
- cotangent: bfloat16 [2048, 2048], P(('fsdp', 'replica')), may hold values from -6 to 6
- ln1: bfloat16 [2, 2048], P('section', 'fsdp'), may hold values from 0.25 to 1.75
- wq: bfloat16 [2, 2048, 2048], P('section', 'fsdp'), may hold values from -0.125 to 0.125
- wk: bfloat16 [2, 2048, 1024], P('section', 'fsdp'), may hold values from -0.125 to 0.125
- wv: bfloat16 [2, 2048, 1024], P('section', 'fsdp'), may hold values from -0.125 to 0.125
- qn: bfloat16 [2, 128], P('section', 'fsdp'), may hold values from 0.5 to 2
- kn: bfloat16 [2, 128], P('section', 'fsdp'), may hold values from 0.5 to 2
- wo: bfloat16 [2, 2048, 2048], P('section', 'fsdp'), may hold values from -0.375 to 0.375
- ln2: bfloat16 [2, 2048], P('section', 'fsdp'), may hold values from 0.25 to 1.75
- wg: bfloat16 [2, 2048, 6144], P('section', 'fsdp'), may hold values from -0.125 to 0.125
- wu: bfloat16 [2, 2048, 6144], P('section', 'fsdp'), may hold values from -0.125 to 0.125
- wd: bfloat16 [2, 6144, 2048], P('section', 'fsdp'), may hold values from -0.078125 to 0.078125
Outputs:
- hidden_out: bfloat16 [2, 2048, 2048], P('section', ('fsdp', 'replica'))
- input_grad: float32 [2, 2048, 2048], P('section', ('fsdp', 'replica'))
- grad_ln1: float32 [2, 2048], P('section', 'fsdp')
- grad_wq: float32 [2, 2048, 2048], P('section', 'fsdp')
- grad_wk: float32 [2, 2048, 1024], P('section', 'fsdp')
- grad_wv: float32 [2, 2048, 1024], P('section', 'fsdp')
- grad_qn: float32 [2, 128], P('section', 'fsdp')
- grad_kn: float32 [2, 128], P('section', 'fsdp')
- grad_wo: float32 [2, 2048, 2048], P('section', 'fsdp')
- grad_ln2: float32 [2, 2048], P('section', 'fsdp')
- grad_wg: float32 [2, 2048, 6144], P('section', 'fsdp')
- up_weight_gradient: float32 [2, 2048, 6144], P('section', 'fsdp')
- grad_wd: float32 [2, 6144, 2048], P('section', 'fsdp')
All inputs are finite; a program needn't handle non-finite values.
Results may differ from a plain program's by a relative error of at most 0.028.
Values may be sent and summed in bfloat16 or wider, within the bound.
A program may use at most 448 MiB of HBM per device.

v0:
```python
import math
import jax
import jax.numpy as jnp
from jax import lax
from jax.sharding import PartitionSpec as P

LEN = 128
EPS = 1e-06


def passed_along(value, axis, steps):
    count = lax.axis_size(axis)
    leading, last = (max(0, -steps), min(count, count - steps))
    return lax.ppermute(value, axis, [(source, source + steps) for source in range(leading, last)])


def rope_tables(length, half_dim):
    freq = jnp.exp(jnp.arange(half_dim, dtype=jnp.float32) * (-math.log(1000000.0) / half_dim))
    angle = jnp.arange(length, dtype=jnp.float32)[:, None] * freq[None, :]
    return (jnp.cos(angle), jnp.sin(angle))


def rotate(field, cosine, sine, sign):
    half_dim = field.shape[-1] // 2
    first = field[..., :half_dim]
    second = field[..., half_dim:]
    cosine = cosine[None, :, None, :]
    sine = sign * sine[None, :, None, :]
    return jnp.concatenate(
        [first * cosine - second * sine, second * cosine + first * sine], axis=-1
    )


def head_norm(field, gain):
    factor = lax.rsqrt(jnp.mean(field * field, axis=-1, keepdims=True) + EPS)
    return (field * factor * gain, factor)


def norm_back(field, factor, gain, grad, axes):
    scaled = grad * gain
    back = factor * scaled - field * factor * factor * factor * jnp.mean(
        scaled * field, axis=-1, keepdims=True
    )
    return (back, jnp.sum(grad * field * factor, axis=axes))


def outer(left, right):
    return lax.dot_general(
        left, right, (((0,), (0,)), ((), ())), preferred_element_type=jnp.float32
    )


def against(left, right):
    return lax.dot_general(
        left, right, (((1,), (1,)), ((), ())), preferred_element_type=jnp.float32
    )


def scores_of(qrot, krot):
    length = qrot.shape[1]
    raw = jnp.einsum("sqkgd,smkd->skgqm", qrot, krot, preferred_element_type=jnp.float32)
    raw = raw * (1.0 / math.sqrt(qrot.shape[-1]))
    causal = jnp.arange(length)[:, None] >= jnp.arange(length)[None, :]
    return jnp.where(causal, raw, -jnp.inf)


def forward_parts(x, weights, length):
    ln1, wq, wk, wv, qn, kn, wo, ln2, wg, wu, wd = weights
    rows = x.shape[0]
    seqs = rows // length
    head_dim = qn.shape[0]
    heads = wq.shape[1] // head_dim
    kv_heads = wk.shape[1] // head_dim
    group = heads // kv_heads
    cosine, sine = rope_tables(length, head_dim // 2)
    x32 = x.astype(jnp.float32)
    r1 = lax.rsqrt(jnp.mean(x32 * x32, axis=-1, keepdims=True) + EPS)
    xn = (x32 * r1 * ln1.astype(jnp.float32)).astype(jnp.bfloat16)
    query = jnp.dot(xn, wq, preferred_element_type=jnp.float32).reshape(
        seqs, length, heads, head_dim
    )
    keys = jnp.dot(xn, wk, preferred_element_type=jnp.float32).reshape(
        seqs, length, kv_heads, head_dim
    )
    values = jnp.dot(xn, wv, preferred_element_type=jnp.float32).astype(jnp.bfloat16)
    q_normed, q_factor = head_norm(query, qn.astype(jnp.float32))
    k_normed, k_factor = head_norm(keys, kn.astype(jnp.float32))
    qrot = (
        rotate(q_normed, cosine, sine, 1.0)
        .astype(jnp.bfloat16)
        .reshape(seqs, length, kv_heads, group, head_dim)
    )
    krot = rotate(k_normed, cosine, sine, 1.0).astype(jnp.bfloat16)
    vals = values.reshape(seqs, length, kv_heads, head_dim)
    scores = scores_of(qrot, krot)
    top = jnp.max(scores, axis=-1, keepdims=True)
    lse = top + jnp.log(jnp.sum(jnp.exp(scores - top), axis=-1, keepdims=True))
    weights_p = jnp.exp(scores - lse).astype(jnp.bfloat16)
    attended = jnp.einsum("skgqm,smkd->sqkgd", weights_p, vals, preferred_element_type=jnp.float32)
    attended = attended.astype(jnp.bfloat16).reshape(rows, heads * head_dim)
    hres = x32 + jnp.dot(attended, wo, preferred_element_type=jnp.float32)
    r2 = lax.rsqrt(jnp.mean(hres * hres, axis=-1, keepdims=True) + EPS)
    hn = (hres * r2 * ln2.astype(jnp.float32)).astype(jnp.bfloat16)
    gate = jnp.dot(hn, wg, preferred_element_type=jnp.float32)
    upper = jnp.dot(hn, wu, preferred_element_type=jnp.float32)
    active = (jax.nn.silu(gate) * upper).astype(jnp.bfloat16)
    output = (hres + jnp.dot(active, wd, preferred_element_type=jnp.float32)).astype(jnp.bfloat16)
    return (
        x32,
        r1,
        xn,
        query,
        q_factor,
        keys,
        k_factor,
        vals,
        qrot,
        krot,
        lse,
        attended,
        hres,
        r2,
        hn,
        gate,
        upper,
        active,
        output,
    )


def blank_parts(x, weights, length):
    ln1, wq, wk, wv, qn, kn, wo, ln2, wg, wu, wd = weights
    rows, width = x.shape
    seqs = rows // length
    head_dim = qn.shape[0]
    heads = wq.shape[1] // head_dim
    kv_heads = wk.shape[1] // head_dim
    group = heads // kv_heads
    hidden = wg.shape[1]
    single = jnp.float32
    narrow = jnp.bfloat16
    return (
        jnp.zeros((rows, width), single),
        jnp.zeros((rows, 1), single),
        jnp.zeros((rows, width), narrow),
        jnp.zeros((seqs, length, heads, head_dim), single),
        jnp.zeros((seqs, length, heads, 1), single),
        jnp.zeros((seqs, length, kv_heads, head_dim), single),
        jnp.zeros((seqs, length, kv_heads, 1), single),
        jnp.zeros((seqs, length, kv_heads, head_dim), narrow),
        jnp.zeros((seqs, length, kv_heads, group, head_dim), narrow),
        jnp.zeros((seqs, length, kv_heads, head_dim), narrow),
        jnp.zeros((seqs, kv_heads, group, length, 1), single),
        jnp.zeros((rows, heads * head_dim), narrow),
        jnp.zeros((rows, width), single),
        jnp.zeros((rows, 1), single),
        jnp.zeros((rows, width), narrow),
        jnp.zeros((rows, hidden), single),
        jnp.zeros((rows, hidden), single),
        jnp.zeros((rows, hidden), narrow),
        jnp.zeros((rows, width), narrow),
    )


def act_backward(parts, grad_out, weights, length):
    ln1, wq, wk, wv, qn, kn, wo, ln2, wg, wu, wd = weights
    (
        x32,
        r1,
        xn,
        query,
        q_factor,
        keys,
        k_factor,
        vals,
        qrot,
        krot,
        lse,
        attended,
        hres,
        r2,
        hn,
        gate,
        upper,
        active,
        output,
    ) = parts
    rows = x32.shape[0]
    seqs = rows // length
    head_dim = qn.shape[0]
    heads = wq.shape[1] // head_dim
    kv_heads = wk.shape[1] // head_dim
    group = heads // kv_heads
    cosine, sine = rope_tables(length, head_dim // 2)
    dact = against(grad_out, wd)
    sig = jax.nn.sigmoid(gate)
    d_up = (dact * gate * sig).astype(jnp.bfloat16)
    d_gate = (dact * upper * sig * (1.0 + gate * (1.0 - sig))).astype(jnp.bfloat16)
    d_hn = against(d_gate, wg) + against(d_up, wu)
    dh_norm, d_ln2 = norm_back(hres, r2, ln2.astype(jnp.float32), d_hn, 0)
    d_h = grad_out.astype(jnp.float32) + dh_norm
    d_ab = d_h.astype(jnp.bfloat16)
    d_out = against(d_ab, wo).astype(jnp.bfloat16).reshape(seqs, length, kv_heads, group, head_dim)
    scores = scores_of(qrot, krot)
    probs = jnp.exp(scores - lse)
    probs_b = probs.astype(jnp.bfloat16)
    d_v = jnp.einsum("skgqm,sqkgd->smkd", probs_b, d_out, preferred_element_type=jnp.float32)
    d_vb = d_v.astype(jnp.bfloat16).reshape(rows, kv_heads * head_dim)
    d_p = jnp.einsum("sqkgd,smkd->skgqm", d_out, vals, preferred_element_type=jnp.float32)
    delta = jnp.sum(probs * d_p, axis=-1, keepdims=True)
    d_s = (probs * (d_p - delta) * (1.0 / math.sqrt(head_dim))).astype(jnp.bfloat16)
    d_qrot = jnp.einsum("skgqm,smkd->sqkgd", d_s, krot, preferred_element_type=jnp.float32).reshape(
        seqs, length, heads, head_dim
    )
    d_krot = jnp.einsum("skgqm,sqkgd->smkd", d_s, qrot, preferred_element_type=jnp.float32)
    d_qh = rotate(d_qrot, cosine, sine, -1.0)
    d_kh = rotate(d_krot, cosine, sine, -1.0)
    d_q, d_qn = norm_back(query, q_factor, qn.astype(jnp.float32), d_qh, (0, 1, 2))
    d_k, d_kn = norm_back(keys, k_factor, kn.astype(jnp.float32), d_kh, (0, 1, 2))
    d_qb = d_q.astype(jnp.bfloat16).reshape(rows, heads * head_dim)
    d_kb = d_k.astype(jnp.bfloat16).reshape(rows, kv_heads * head_dim)
    d_xn = against(d_qb, wq) + against(d_kb, wk) + against(d_vb, wv)
    dx_norm, d_ln1 = norm_back(x32, r1, ln1.astype(jnp.float32), d_xn, 0)
    d_x = d_h + dx_norm
    saved = (xn, d_qb, d_kb, d_vb, attended, d_ab, hn, d_gate, d_up, active, grad_out)
    return (d_x, saved, (d_ln1, d_qn, d_kn, d_ln2))


def blank_backward(x, weights):
    ln1, wq, wk, wv, qn, kn, wo, ln2, wg, wu, wd = weights
    rows, width = x.shape

    def empty(columns):
        return jnp.zeros((rows, columns), jnp.bfloat16)

    saved = (
        empty(width),
        empty(wq.shape[1]),
        empty(wk.shape[1]),
        empty(wv.shape[1]),
        empty(wq.shape[1]),
        empty(width),
        empty(width),
        empty(wg.shape[1]),
        empty(wg.shape[1]),
        empty(wg.shape[1]),
        empty(width),
    )
    small = (
        jnp.zeros((width,), jnp.float32),
        jnp.zeros((qn.shape[0],), jnp.float32),
        jnp.zeros((qn.shape[0],), jnp.float32),
        jnp.zeros((width,), jnp.float32),
    )
    return (jnp.zeros((rows, width), jnp.float32), saved, small)


def per_device(tokens_in, cotangent, ln1, wq, wk, wv, qn, kn, wo, ln2, wg, wu, wd):
    relay_section = lax.axis_index("section")
    shards = (ln1[0], wq[0], wk[0], wv[0], qn[0], kn[0], wo[0], ln2[0], wg[0], wu[0], wd[0])
    gathered = (
        lax.all_gather(shards[0], "fsdp", axis=0, tiled=True),
        lax.all_gather(shards[1], "fsdp", axis=0, tiled=True),
        lax.all_gather(shards[2], "fsdp", axis=0, tiled=True),
        lax.all_gather(shards[3], "fsdp", axis=0, tiled=True),
        lax.all_gather(shards[4], "fsdp", axis=0, tiled=True),
        lax.all_gather(shards[5], "fsdp", axis=0, tiled=True),
        lax.all_gather(shards[6], "fsdp", axis=0, tiled=True),
        lax.all_gather(shards[7], "fsdp", axis=0, tiled=True),
        lax.all_gather(shards[8], "fsdp", axis=0, tiled=True),
        lax.all_gather(shards[9], "fsdp", axis=0, tiled=True),
        lax.all_gather(shards[10], "fsdp", axis=0, tiled=True),
    )

    def forward_execute(layer_in):
        return forward_parts(layer_in, gathered, LEN)

    def skip_forward(layer_in):
        return blank_parts(layer_in, gathered, LEN)

    first_parts = lax.cond(relay_section == 0, forward_execute, skip_forward, tokens_in)
    first = first_parts[-1]
    passed = passed_along(first, "section", 1)
    second_parts = lax.cond(relay_section == 1, forward_execute, skip_forward, passed)
    hidden_out = jnp.where(relay_section == 0, first, second_parts[-1])

    def run_backward(pair):
        return act_backward(pair[0], pair[1], gathered, LEN)

    def skip_backward(pair):
        return blank_backward(pair[0][0], gathered)

    late = lax.cond(relay_section == 1, run_backward, skip_backward, (second_parts, cotangent))
    sent = passed_along(late[0].astype(jnp.bfloat16), "section", -1)
    early = lax.cond(relay_section == 0, run_backward, skip_backward, (first_parts, sent))
    picked = jax.tree.map(
        lambda left, right: jnp.where(relay_section == 0, left, right), early, late
    )
    input_grad = picked[0]
    xn, d_qb, d_kb, d_vb, attended, d_ab, hn, d_gate, d_up, active, grad_out = picked[1]
    d_ln1, d_qn, d_kn, d_ln2 = picked[2]
    lefts = (
        lax.all_to_all(xn, "fsdp", split_axis=1, concat_axis=0, tiled=True),
        lax.all_to_all(attended, "fsdp", split_axis=1, concat_axis=0, tiled=True),
        lax.all_to_all(hn, "fsdp", split_axis=1, concat_axis=0, tiled=True),
        lax.all_to_all(active, "fsdp", split_axis=1, concat_axis=0, tiled=True),
    )
    rights = (
        lax.all_gather(d_qb, "fsdp", axis=0, tiled=True),
        lax.all_gather(d_kb, "fsdp", axis=0, tiled=True),
        lax.all_gather(d_vb, "fsdp", axis=0, tiled=True),
        lax.all_gather(d_ab, "fsdp", axis=0, tiled=True),
        lax.all_gather(d_gate, "fsdp", axis=0, tiled=True),
        lax.all_gather(d_up, "fsdp", axis=0, tiled=True),
        lax.all_gather(grad_out, "fsdp", axis=0, tiled=True),
    )
    gains = (
        lax.psum_scatter(d_ln1, "fsdp", scatter_dimension=0, tiled=True),
        lax.psum_scatter(d_qn, "fsdp", scatter_dimension=0, tiled=True),
        lax.psum_scatter(d_kn, "fsdp", scatter_dimension=0, tiled=True),
        lax.psum_scatter(d_ln2, "fsdp", scatter_dimension=0, tiled=True),
    )
    local = (
        gains[0],
        outer(lefts[0], rights[0]),
        outer(lefts[0], rights[1]),
        outer(lefts[0], rights[2]),
        gains[1],
        gains[2],
        outer(lefts[1], rights[3]),
        gains[3],
        outer(lefts[2], rights[4]),
        outer(lefts[2], rights[5]),
        outer(lefts[3], rights[6]),
    )
    owned = (
        lax.psum(local[0].astype(jnp.bfloat16), "replica").astype(jnp.float32),
        lax.psum(local[1].astype(jnp.bfloat16), "replica").astype(jnp.float32),
        lax.psum(local[2].astype(jnp.bfloat16), "replica").astype(jnp.float32),
        lax.psum(local[3].astype(jnp.bfloat16), "replica").astype(jnp.float32),
        lax.psum(local[4].astype(jnp.bfloat16), "replica").astype(jnp.float32),
        lax.psum(local[5].astype(jnp.bfloat16), "replica").astype(jnp.float32),
        lax.psum(local[6].astype(jnp.bfloat16), "replica").astype(jnp.float32),
        lax.psum(local[7].astype(jnp.bfloat16), "replica").astype(jnp.float32),
        lax.psum(local[8].astype(jnp.bfloat16), "replica").astype(jnp.float32),
        lax.psum(local[9].astype(jnp.bfloat16), "replica").astype(jnp.float32),
        lax.psum(local[10].astype(jnp.bfloat16), "replica").astype(jnp.float32),
    )
    return (
        hidden_out[None],
        input_grad[None],
        owned[0][None],
        owned[1][None],
        owned[2][None],
        owned[3][None],
        owned[4][None],
        owned[5][None],
        owned[6][None],
        owned[7][None],
        owned[8][None],
        owned[9][None],
        owned[10][None],
    )


def solution(mesh):
    return jax.shard_map(
        per_device,
        mesh=mesh,
        in_specs=(
            P(("fsdp", "replica"), None),
            P(("fsdp", "replica"), None),
            P("section", "fsdp"),
            P("section", "fsdp", None),
            P("section", "fsdp", None),
            P("section", "fsdp", None),
            P("section", "fsdp"),
            P("section", "fsdp"),
            P("section", "fsdp", None),
            P("section", "fsdp"),
            P("section", "fsdp", None),
            P("section", "fsdp", None),
            P("section", "fsdp", None),
        ),
        out_specs=(
            P("section", ("fsdp", "replica"), None),
            P("section", ("fsdp", "replica"), None),
            P("section", "fsdp"),
            P("section", "fsdp", None),
            P("section", "fsdp", None),
            P("section", "fsdp", None),
            P("section", "fsdp"),
            P("section", "fsdp"),
            P("section", "fsdp", None),
            P("section", "fsdp"),
            P("section", "fsdp", None),
            P("section", "fsdp", None),
            P("section", "fsdp", None),
        ),
        check_vma=False,
    )
```

profile of v0, /device:TPU:0, one launch (start us, length us, event | category | flops | bytes accessed | tf_op | source)
XLA Modules:
  0.0 3080.5 jit_solution(9624293792412232464)
XLA Ops:
  50.7 42.8 %all-gather.42.cloned.1.call-done = bf16[1,2048,1024]{2,1,0:T(8,128)(2,1)} async-done(((bf16[1,512,1024]{2,1,0:T(8,128)(2,1)}), bf16[1,2048,1024]{2,1,0:T(8,128)(2,1)}) %all-gather.42.cloned.1.call-update) | async-done | bytes 4194320 | tf_op jit(solution)/shard_map/all_gather | solution.py:264
  93.4 80.9 %all-gather.44.cloned.1.call-done = bf16[1,2048,1024]{2,1,0:T(8,128)(2,1)} async-done(((bf16[1,512,1024]{2,1,0:T(8,128)(2,1)}), bf16[1,2048,1024]{2,1,0:T(8,128)(2,1)}) %all-gather.44.cloned.1.call-update) | async-done | bytes 4194320 | tf_op jit(solution)/shard_map/all_gather | solution.py:265
  174.3 149.7 %all-gather.40.cloned.1.call-done = bf16[1,2048,2048]{2,1,0:T(8,128)(2,1)} async-done(((bf16[1,512,2048]{2,1,0:T(8,128)(2,1)}), bf16[1,2048,2048]{2,1,0:T(8,128)(2,1)}) %all-gather.40.cloned.1.call-update) | async-done | bytes 8388624 | tf_op jit(solution)/shard_map/all_gather | solution.py:263
  324.0 149.3 %all-gather.46.cloned.1.call-done = bf16[1,2048,2048]{2,1,0:T(8,128)(2,1)} async-done(((bf16[1,512,2048]{2,1,0:T(8,128)(2,1)}), bf16[1,2048,2048]{2,1,0:T(8,128)(2,1)}) %all-gather.46.cloned.1.call-update) | async-done | bytes 8388624 | tf_op jit(solution)/shard_map/all_gather | solution.py:268
  473.3 424.8 %all-gather.48.cloned.1.call-done = bf16[1,2048,6144]{2,1,0:T(8,128)(2,1)} async-done(((bf16[1,512,6144]{2,1,0:T(8,128)(2,1)}), bf16[1,2048,6144]{2,1,0:T(8,128)(2,1)}) %all-gather.48.cloned.1.call-update) | async-done | bytes 25165840 | tf_op jit(solution)/shard_map/all_gather | solution.py:270
  898.1 424.8 %all-gather.50.cloned.1.call-done = bf16[1,2048,6144]{2,1,0:T(8,128)(2,1)} async-done(((bf16[1,512,6144]{2,1,0:T(8,128)(2,1)}), bf16[1,2048,6144]{2,1,0:T(8,128)(2,1)}) %all-gather.50.cloned.1.call-update) | async-done | bytes 25165840 | tf_op jit(solution)/shard_map/all_gather | solution.py:271
  1322.9 425.0 %all-gather.52.cloned.1.call-done = bf16[1,6144,2048]{2,1,0:T(8,128)(2,1)} async-done(((bf16[1,1536,2048]{2,1,0:T(8,128)(2,1)}), bf16[1,6144,2048]{2,1,0:T(8,128)(2,1)}) %all-gather.52.cloned.1.call-update) | async-done | bytes 25165840 | tf_op jit(solution)/shard_map/all_gather | solution.py:272
  1747.8 67.8 %conditional.4 = (f32[128,2048]{1,0:T(8,128)S(1)}, f32[128,1]{0,1:T(1,128)S(1)}, bf16[128,2048]{1,0:T(8,128)(2,1)}, f32[1,128,16,128]{3,2,1,0:T(8,128)S(1)}, f32...) conditional(s32[]{:T(128)} %convert_element_type.277, () %tuple.40, ...), branch_computations={%region_0.0_spmd, %region_1.8_spmd} | conditional | flops 13036057600 | bytes 192852512 | solution.py:281
  1785.8 15.1 multiply_convert_fusion
  1818.8 25.6 conditional.5
  1844.9 23.1 conditional.6
  1869.4 161.2 %collective-permute-done.1 = bf16[128,2048]{1,0:T(8,128)(2,1)} collective-permute-done((bf16[128,2048]{1,0:T(8,128)(2,1)S(1)}, bf16[128,2048]{1,0:T(8,128)(2,1)}, u32[]{:S(2)}, u32[]{:S(2)}) %collective-permute-start.1) | collective-permute-done | bytes 524320 | tf_op jit(solution)/shard_map/ppermute | solution.py:14
  2030.6 108.4 %conditional.7 = (bf16[128,2048]{0,1:T(8,128)(2,1)}, bf16[128,1024]{0,1:T(8,128)(2,1)}, bf16[128,1024]{0,1:T(8,128)(2,1)}, f32[2048]{0:T(1024)S(1)}, f32[128]{0:...) conditional(s32[]{:T(128)} %convert_element_type.277, () %tuple.44, ...), branch_computations={%region_27.28_spmd, %region_28.38_spmd} | conditional | flops 13252196352 | bytes 250843936 | solution.py:295
  2032.0 15.8 multiply_convert_fusion.9
  2047.8 14.1 fusion.88
  2061.9 15.0 multiply_reduce_fusion.17
  2179.1 17.4 all-to-all-done.1
  2225.0 43.9 %all-to-all-done.3 = bf16[128,4,1536]{0,2,1:T(8,128)(2,1)S(1)} async-done(((bf16[128,4,1536]{0,2,1:T(8,128)(2,1)}), bf16[128,4,1536]{0,2,1:T(8,128)(2,1)S(1)}, u32[]{:S(2)}, u32[]{:S(2)}) %all-to-all-start.3) | async-done | bytes 1572896 | tf_op jit(solution)/shard_map/all_to_all | solution.py:306
  2275.6 42.4 %all-gather.32.cloned.1.call-done = bf16[512,2048]{0,1:T(8,128)(2,1)} async-done(((bf16[128,2048]{0,1:T(8,128)(2,1)}), bf16[512,2048]{0,1:T(8,128)(2,1)}) %all-gather.32.cloned.1.call-update) | async-done | bytes 2097168 | tf_op jit(solution)/shard_map/all_gather | solution.py:312
  2322.2 41.7 %all-gather.38.cloned.1.call-done = bf16[512,2048]{0,1:T(8,128)(2,1)} async-done(((bf16[128,2048]{0,1:T(8,128)(2,1)}), bf16[512,2048]{0,1:T(8,128)(2,1)}) %all-gather.38.cloned.1.call-update) | async-done | bytes 2097168 | tf_op jit(solution)/shard_map/all_gather | solution.py:315
  2370.9 108.1 %all-gather.34.cloned.1.call-done = bf16[512,6144]{0,1:T(8,128)(2,1)} async-done(((bf16[128,6144]{0,1:T(8,128)(2,1)}), bf16[512,6144]{0,1:T(8,128)(2,1)}) %all-gather.34.cloned.1.call-update) | async-done | bytes 6291472 | tf_op jit(solution)/shard_map/all_gather | solution.py:313
  2487.3 106.8 %all-gather.36.cloned.1.call-done = bf16[512,6144]{0,1:T(8,128)(2,1)} async-done(((bf16[128,6144]{0,1:T(8,128)(2,1)}), bf16[512,6144]{0,1:T(8,128)(2,1)}) %all-gather.36.cloned.1.call-update) | async-done | bytes 6291472 | tf_op jit(solution)/shard_map/all_gather | solution.py:314
  2608.2 16.7 all-reduce.6
  2637.7 406.8 %all-reduce.12.cloned.1.call-done = (bf16[1,512,2048]{2,1,0:T(8,128)(2,1)}, bf16[1,512,1024]{2,1,0:T(8,128)(2,1)}, bf16[1,512,1024]{2,1,0:T(8,128)(2,1)}, bf16[1...) async-done(((bf16[1,512,2048]{2,1,0:T(8,128)(2,1)}, bf16[1,512,1024]{2,1,0:T(8,128)(2,1)}, ...) | async-done | bytes 25165840 | tf_op jit(solution)/shard_map/psum | solution.py:338
  (358 shorter events, 340.0 us)
Async XLA Ops:
  7.2 86.2 %all-gather.42.cloned.1.call-start = ((), (), s32[]{:S(2)}) async-start(), calls=%async_computation.12 | async-start | bytes 5242880 | tf_op jit(solution)/shard_map/all_gather | solution.py:264
  7.9 166.4 %all-gather.44.cloned.1.call-start = ((), (), s32[]{:S(2)}) async-start(), calls=%async_computation.13 | async-start | bytes 5242880 | tf_op jit(solution)/shard_map/all_gather | solution.py:265
  8.7 315.3 %all-gather.40.cloned.1.call-start = ((), (), s32[]{:S(2)}) async-start(), calls=%async_computation.11 | async-start | bytes 10485760 | tf_op jit(solution)/shard_map/all_gather | solution.py:263
  9.4 463.9 %all-gather.46.cloned.1.call-start = ((), (), s32[]{:S(2)}) async-start(), calls=%async_computation.14 | async-start | bytes 10485760 | tf_op jit(solution)/shard_map/all_gather | solution.py:268
  10.0 888.1 %all-gather.48.cloned.1.call-start = ((), (), s32[]{:S(2)}) async-start(), calls=%async_computation.15 | async-start | bytes 31457280 | tf_op jit(solution)/shard_map/all_gather | solution.py:270
  10.6 1312.3 %all-gather.50.cloned.1.call-start = ((), (), s32[]{:S(2)}) async-start(), calls=%async_computation.16 | async-start | bytes 31457280 | tf_op jit(solution)/shard_map/all_gather | solution.py:271
  11.2 1736.6 %copy-start.50 = (bf16[128,2048]{1,0:T(8,128)(2,1)S(1)}, bf16[128,2048]{1,0:T(8,128)(2,1)}, u32[]{:S(2)}) copy-start(bf16[128,2048]{1,0:T(8,128)(2,1)} %param.21) | copy-start | bytes 1572868
  11.2 1736.6 %all-gather.52.cloned.1.call-start = ((), (), s32[]{:S(2)}) async-start(), calls=%async_computation.17 | async-start | bytes 31457280 | tf_op jit(solution)/shard_map/all_gather | solution.py:272
  11.9 2206.9 %all-gather.28.cloned.1.call-start = ((), (), s32[]{:S(2)}) async-start(), calls=%async_computation.5 | async-start | bytes 1310720 | tf_op jit(solution)/shard_map/all_gather | solution.py:310
  50.7 1768.1 %copy-start.87 = (bf16[128]{0:T(256)(128)(2,1)}, bf16[128]{0:T(256)(128)(2,1)S(1)}, u32[]{:S(2)}) copy-start(bf16[128]{0:T(256)(128)(2,1)S(1)} %get-tuple-element.1148) | copy-start | bytes 772
  50.7 1768.1 %copy-start.90 = (bf16[128]{0:T(256)(128)(2,1)}, bf16[128]{0:T(256)(128)(2,1)S(1)}, u32[]{:S(2)}) copy-start(bf16[128]{0:T(256)(128)(2,1)S(1)} %get-tuple-element.1149) | copy-start | bytes 772
  1815.7 3.0 collective-permute-start
  1868.1 162.5 %collective-permute-start.1 = (bf16[128,2048]{1,0:T(8,128)(2,1)S(1)}, bf16[128,2048]{1,0:T(8,128)(2,1)}, u32[]{:S(2)}, u32[]{:S(2)}) collective-permute-start(bf16[128,2048]{1,0:T(8,128)(2,1)S(1)} %convert_element_type.279), channel_id=1, source_target_pairs={{16,0},{17,1},{18,2},{19,3},{20,4},{21,5},{22,6},{23,7},{24,8},{25... | collective-permute-start | bytes 1572872 | tf_op jit(solution)/shard_map/ppermute | solution.py:14
  2140.7 81.3 %all-gather.30.cloned.1.call-start = ((), (), s32[]{:S(2)}) async-start(), calls=%async_computation.6 | async-start | bytes 1310720 | tf_op jit(solution)/shard_map/all_gather | solution.py:311
  2142.5 128.7 %all-gather.26.cloned.1.call-start = ((), (), s32[]{:S(2)}) async-start(), calls=%async_computation.4 | async-start | bytes 2621440 | tf_op jit(solution)/shard_map/all_gather | solution.py:309
  2144.5 173.5 %all-gather.32.cloned.1.call-start = ((), (), s32[]{:S(2)}) async-start(), calls=%async_computation.7 | async-start | bytes 2621440 | tf_op jit(solution)/shard_map/all_gather | solution.py:312
  2146.5 217.4 %all-gather.38.cloned.1.call-start = ((), (), s32[]{:S(2)}) async-start(), calls=%async_computation.10 | async-start | bytes 2621440 | tf_op jit(solution)/shard_map/all_gather | solution.py:315
  2148.5 330.6 %all-gather.34.cloned.1.call-start = ((), (), s32[]{:S(2)}) async-start(), calls=%async_computation.8 | async-start | bytes 7864320 | tf_op jit(solution)/shard_map/all_gather | solution.py:313
  2151.3 442.8 %all-gather.36.cloned.1.call-start = ((), (), s32[]{:S(2)}) async-start(), calls=%async_computation.9 | async-start | bytes 7864320 | tf_op jit(solution)/shard_map/all_gather | solution.py:314
  2156.0 17.7 all-to-all-start
  2173.7 22.8 all-to-all-start.1
  2196.5 15.7 all-to-all-start.2
  2212.2 56.8 %all-to-all-start.3 = ((bf16[128,4,1536]{0,2,1:T(8,128)(2,1)}), bf16[128,4,1536]{0,2,1:T(8,128)(2,1)S(1)}, u32[]{:S(2)}, u32[]{:S(2)}) async-start(bf16[128,4,1536]{0,2,1:T(8,128)(2,1)} %bitcast.171), calls=%async_computation.3 | async-start | bytes 3145728 | tf_op jit(solution)/shard_map/all_to_all | solution.py:306
  2215.7 828.7 %all-reduce.12.cloned.1.call-start = ((), (), s32[]{:S(2)}) async-start(), calls=%async_computation.18 | async-start | bytes 50331648 | tf_op jit(solution)/shard_map/psum | solution.py:338
  (66 other events, 914.7 us)
Sparse Core Ops, SparseCore 0:
  9.6 83.8 all-gather.41
  95.0 79.2 all-gather.43
  175.9 148.0 all-gather.39
  325.4 147.7 all-gather.45
  474.7 423.3 all-gather.47
  899.5 423.3 all-gather.49
  1324.5 423.3 all-gather.51
  2140.9 31.9 all-gather.27
  2174.4 34.9 all-gather.29
  2211.4 59.7 all-gather.25
  2272.7 45.2 all-gather.31
  2319.4 44.4 all-gather.37
  2366.0 112.9 all-gather.33
  2481.1 112.9 all-gather.35
  2602.4 441.9 all-reduce.11
where the time goes:
time: 3090 us; the launch traced here: 3080 us
  waiting for transfers between devices  2660 us (86%)
  matrix products  167 us (5%)
  other arithmetic  75.6 us (2%)
  blocking collectives  63.8 us (2%)
  local copies, waits for them, and re-layouts  62.9 us (2%)
    all_gather x1, waiting for transfers between devices, per_device(): lax.all_gather(shards[10], 'fsdp', axis=0, tiled=True)  425 us
    all_gather x1, waiting for transfers between devices, per_device(): lax.all_gather(shards[9], 'fsdp', axis=0, tiled=True)  425 us
    all_gather x1, waiting for transfers between devices, per_device(): lax.all_gather(shards[8], 'fsdp', axis=0, tiled=True)  425 us
    psum x1, waiting for transfers between devices, per_device(): lax.psum(local[1].astype(jnp.bfloat16), 'replica').astype(jnp.float32)  407 us
    ppermute x2, waiting for transfers between devices, passed_along(): lax.ppermute(value, axis, [(source, source + steps) for source in range(l...  163 us
    all_gather x1, waiting for transfers between devices, per_device(): lax.all_gather(shards[1], 'fsdp', axis=0, tiled=True)  150 us
    all_gather x1, waiting for transfers between devices, per_device(): lax.all_gather(shards[6], 'fsdp', axis=0, tiled=True)  149 us
    all_gather x1, waiting for transfers between devices, per_device(): lax.all_gather(d_gate, 'fsdp', axis=0, tiled=True)  108 us
  transfers between devices with their start and end apart: 21, of which 19 were waited for; matrix products, arithmetic and copies ran while one was open for 2% of the time, Pallas kernels for 0%

commit v1 on v0

--- a/solution.py
+++ b/solution.py
@@ -6,6 +6,19 @@
 
 LEN = 128
 EPS = 1e-06
+
+
+def collect(array, axis, dim):
+    ways = lax.axis_size(axis)
+    up = [(d, (d + 1) % ways) for d in range(ways)]
+    down = [(d, (d - 1) % ways) for d in range(ways)]
+    earlier, later = ([array], [array])
+    for _ in range(ways // 2):
+        earlier.append(lax.ppermute(earlier[-1], axis, up))
+    for _ in range((ways - 1) // 2):
+        later.append(lax.ppermute(later[-1], axis, down))
+    line = jnp.concatenate([*earlier[::-1], *later[1:]], axis=dim)
+    return jnp.roll(line, (lax.axis_index(axis) - ways // 2) * array.shape[dim], axis=dim)
 
 
 def passed_along(value, axis, steps):
@@ -269,7 +282,7 @@
         lax.all_gather(shards[7], "fsdp", axis=0, tiled=True),
         lax.all_gather(shards[8], "fsdp", axis=0, tiled=True),
         lax.all_gather(shards[9], "fsdp", axis=0, tiled=True),
-        lax.all_gather(shards[10], "fsdp", axis=0, tiled=True),
+        collect(shards[10], "fsdp", 0),
     )
 
     def forward_execute(layer_in):

time: 3090 us -> 3030 us (0.981)
  waiting for transfers between devices: 2660 us -> 1980 us
  blocking collectives: 63.8 us -> 576 us
  local copies, waits for them, and re-layouts: 62.9 us -> 135 us
    all_gather x1, blocking collectives: 13.8 us -> 518 us  [per_device(): lax.all_gather(shards[0], 'fsdp', axis=0, tiled=True)]
    all_gather x1 -> x0, waiting for transfers between devices: 425 us -> none  [per_device(): lax.all_gather(shards[10], 'fsdp', axis=0, tiled=True)]
    ppermute x0 -> x3, waiting for transfers between devices: none -> 253 us  [the longest x2 253 us: collect(): earlier.append(lax.ppermute(earlier[-1], axis, up))]
    all_gather x1, waiting for transfers between devices: 150 us -> 0.01 us  [per_device(): lax.all_gather(shards[1], 'fsdp', axis=0, tiled=True)]
    all_gather x1, waiting for transfers between devices: 149 us -> 0.01 us  [per_device(): lax.all_gather(shards[6], 'fsdp', axis=0, tiled=True)]
    all_gather x1, waiting for transfers between devices: 80.9 us -> 0.01 us  [per_device(): lax.all_gather(shards[3], 'fsdp', axis=0, tiled=True)]
    all_gather x1, waiting for transfers between devices: 425 us -> 345 us  [per_device(): lax.all_gather(shards[8], 'fsdp', axis=0, tiled=True)]
    all_gather x1, waiting for transfers between devices: 42.8 us -> 0.01 us  [per_device(): lax.all_gather(shards[2], 'fsdp', axis=0, tiled=True)]
  transfers between devices with their start and end apart: 21 -> 23, of which waited for: 19 -> 15; matrix products, arithmetic and copies ran while one was open for 2% -> 4% of each run, Pallas kernels for 0% -> 0%
where the time goes in v1:
time: 3030 us; the launch traced here: 3020 us
  waiting for transfers between devices  1980 us (65%)
  blocking collectives  576 us (19%)
  matrix products  168 us (6%)
  local copies, waits for them, and re-layouts  135 us (4%)
  other arithmetic  85.7 us (3%)
  starting transfers between devices  42.8 us (1%)
    all_gather x1, blocking collectives, per_device(): lax.all_gather(shards[0], 'fsdp', axis=0, tiled=True)  518 us
    all_gather x1, waiting for transfers between devices, per_device(): lax.all_gather(shards[9], 'fsdp', axis=0, tiled=True)  425 us
    psum x1, waiting for transfers between devices, per_device(): lax.psum(local[1].astype(jnp.bfloat16), 'replica').astype(jnp.float32)  405 us
    all_gather x1, waiting for transfers between devices, per_device(): lax.all_gather(shards[8], 'fsdp', axis=0, tiled=True)  345 us
    ppermute x2, waiting for transfers between devices, collect(): earlier.append(lax.ppermute(earlier[-1], axis, up))  253 us
    ppermute x2, waiting for transfers between devices, passed_along(): lax.ppermute(value, axis, [(source, source + steps) for source in range(l...  159 us
    all_gather x1, waiting for transfers between devices, per_device(): lax.all_gather(d_up, 'fsdp', axis=0, tiled=True)  108 us
    all_gather x1, waiting for transfers between devices, per_device(): lax.all_gather(d_gate, 'fsdp', axis=0, tiled=True)  107 us
  transfers between devices with their start and end apart: 23, of which 15 were waited for; matrix products, arithmetic and copies ran while one was open for 4% of the time, Pallas kernels for 0%

profile of v1, /device:TPU:0, one launch (start us, length us, event | category | flops | bytes accessed | tf_op | source)
XLA Modules:
  0.0 3020.7 jit_solution(362967003791450053)
XLA Ops:
  14.3 252.7 %collective-permute-done = bf16[1536,2048]{1,0:T(8,128)(2,1)} collective-permute-done((bf16[1536,2048]{1,0:T(8,128)(2,1)}, bf16[1536,2048]{1,0:T(8,128)(2,1)}, u32[]{:S(2)}, u32[]{:S(2)}) %collective-permute-start) | collective-permute-done | bytes 6291488 | tf_op jit(solution)/shard_map/ppermute | solution.py:17
  267.1 18.7 collective-permute-start.1
  288.8 517.9 %all-gather = bf16[1,2048]{1,0:T(2,128)(2,1)S(1)} all-gather(bf16[1,512]{1,0:T(2,128)(2,1)S(1)} %copy-done.87), channel_id=2, replica_groups=mesh['section'=2,'fsdp'=4,'replica'=4] {'fsdp'}, dimensions={1}, use_global_device_ids=true | all-gather | bytes 5120 | tf_op jit(solution)/shard_map/all_gather | solution.py:275
  806.7 21.1 all-gather.7
  887.7 22.5 constant_dynamic-slice_fusion
  910.2 344.7 %all-gather.46.cloned.1.call-done = bf16[1,2048,6144]{2,1,0:T(8,128)(2,1)} async-done(((bf16[1,512,6144]{2,1,0:T(8,128)(2,1)}), bf16[1,2048,6144]{2,1,0:T(8,128)(2,1)}) %all-gather.46.cloned.1.call-update) | async-done | bytes 25165840 | tf_op jit(solution)/shard_map/all_gather | solution.py:283
  1254.9 424.8 %all-gather.48.cloned.1.call-done = bf16[1,2048,6144]{2,1,0:T(8,128)(2,1)} async-done(((bf16[1,512,6144]{2,1,0:T(8,128)(2,1)}), bf16[1,2048,6144]{2,1,0:T(8,128)(2,1)}) %all-gather.48.cloned.1.call-update) | async-done | bytes 25165840 | tf_op jit(solution)/shard_map/all_gather | solution.py:284
  1679.7 71.1 %conditional.4 = (f32[128,2048]{1,0:T(8,128)S(1)}, f32[128,1]{0,1:T(1,128)S(1)}, bf16[128,2048]{1,0:T(8,128)(2,1)}, f32[1,128,16,128]{3,2,1,0:T(8,128)}, f32[1,1...) conditional(s32[]{:T(128)} %convert_element_type.277, () %tuple.40, ...), branch_computations={%region_0.1_spmd, %region_1.8_spmd} | conditional | flops 13036057600 | bytes 205435584 | solution.py:294
  1717.1 15.5 multiply_convert_fusion
  1754.0 23.1 conditional.5
  1777.8 22.9 conditional.6
  1802.2 157.5 %collective-permute-done.4 = bf16[128,2048]{1,0:T(8,128)(2,1)} collective-permute-done((bf16[128,2048]{1,0:T(8,128)(2,1)S(1)}, bf16[128,2048]{1,0:T(8,128)(2,1)}, u32[]{:S(2)}, u32[]{:S(2)}) %collective-permute-start.4) | collective-permute-done | bytes 524320 | tf_op jit(solution)/shard_map/ppermute | solution.py:27
  1959.7 116.3 %conditional.7 = (bf16[128,2048]{0,1:T(8,128)(2,1)}, bf16[128,1024]{0,1:T(8,128)(2,1)}, bf16[128,1024]{0,1:T(8,128)(2,1)}, f32[2048]{0:T(1024)}, f32[128]{0:T(12...) conditional(s32[]{:T(128)} %convert_element_type.277, () %tuple.44, ...), branch_computations={%region_27.28_spmd, %region_28.38_spmd} | conditional | flops 13252196352 | bytes 241408736 | solution.py:308
  1959.7 16.1 multiply_convert_fusion.9
  1975.8 14.3 fusion.88
  1990.1 14.9 multiply_reduce_fusion.17
  2116.0 16.5 all-to-all-done.1
  2161.4 35.7 %all-to-all-done.3 = bf16[128,4,1536]{0,2,1:T(8,128)(2,1)S(1)} async-done(((bf16[128,4,1536]{0,2,1:T(8,128)(2,1)}), bf16[128,4,1536]{0,2,1:T(8,128)(2,1)S(1)}, u32[]{:S(2)}, u32[]{:S(2)}) %all-to-all-start.3) | async-done | bytes 1572896 | tf_op jit(solution)/shard_map/all_to_all | solution.py:319
  2213.7 43.3 %all-gather.30.cloned.1.call-done = bf16[512,2048]{0,1:T(8,128)(2,1)} async-done(((bf16[128,2048]{0,1:T(8,128)(2,1)}), bf16[512,2048]{0,1:T(8,128)(2,1)}) %all-gather.30.cloned.1.call-update) | async-done | bytes 2097168 | tf_op jit(solution)/shard_map/all_gather | solution.py:325
  2261.3 41.8 %all-gather.36.cloned.1.call-done = bf16[512,2048]{0,1:T(8,128)(2,1)} async-done(((bf16[128,2048]{0,1:T(8,128)(2,1)}), bf16[512,2048]{0,1:T(8,128)(2,1)}) %all-gather.36.cloned.1.call-update) | async-done | bytes 2097168 | tf_op jit(solution)/shard_map/all_gather | solution.py:328
  2310.1 108.0 %all-gather.34.cloned.1.call-done = bf16[512,6144]{0,1:T(8,128)(2,1)} async-done(((bf16[128,6144]{0,1:T(8,128)(2,1)}), bf16[512,6144]{0,1:T(8,128)(2,1)}) %all-gather.34.cloned.1.call-update) | async-done | bytes 6291472 | tf_op jit(solution)/shard_map/all_gather | solution.py:327
  2426.3 107.0 %all-gather.32.cloned.1.call-done = bf16[512,6144]{0,1:T(8,128)(2,1)} async-done(((bf16[128,6144]{0,1:T(8,128)(2,1)}), bf16[512,6144]{0,1:T(8,128)(2,1)}) %all-gather.32.cloned.1.call-update) | async-done | bytes 6291472 | tf_op jit(solution)/shard_map/all_gather | solution.py:326
  2546.8 16.6 all-reduce.6
  2579.0 404.6 %all-reduce.12.cloned.1.call-done = (bf16[1,512,2048]{2,1,0:T(8,128)(2,1)}, bf16[1,512,1024]{2,1,0:T(8,128)(2,1)}, bf16[1,512,1024]{2,1,0:T(8,128)(2,1)}, bf16[1...) async-done(((bf16[1,512,2048]{2,1,0:T(8,128)(2,1)}, bf16[1,512,1024]{2,1,0:T(8,128)(2,1)}, ...) | async-done | bytes 25165840 | tf_op jit(solution)/shard_map/psum | solution.py:351
  (381 shorter events, 389.2 us)
Async XLA Ops:
  7.2 903.0 %all-gather.40.cloned.1.call-start = ((), (), s32[]{:S(2)}) async-start(), calls=%async_computation.12 | async-start | bytes 5242880 | tf_op jit(solution)/shard_map/all_gather | solution.py:277
  7.9 902.3 %all-gather.42.cloned.1.call-start = ((), (), s32[]{:S(2)}) async-start(), calls=%async_computation.13 | async-start | bytes 5242880 | tf_op jit(solution)/shard_map/all_gather | solution.py:278
  8.7 901.5 %all-gather.38.cloned.1.call-start = ((), (), s32[]{:S(2)}) async-start(), calls=%async_computation.11 | async-start | bytes 10485760 | tf_op jit(solution)/shard_map/all_gather | solution.py:276
  9.4 900.8 %all-gather.44.cloned.1.call-start = ((), (), s32[]{:S(2)}) async-start(), calls=%async_computation.14 | async-start | bytes 10485760 | tf_op jit(solution)/shard_map/all_gather | solution.py:281
  10.0 1244.9 %all-gather.46.cloned.1.call-start = ((), (), s32[]{:S(2)}) async-start(), calls=%async_computation.15 | async-start | bytes 31457280 | tf_op jit(solution)/shard_map/all_gather | solution.py:283
  10.6 1669.1 %all-gather.48.cloned.1.call-start = ((), (), s32[]{:S(2)}) async-start(), calls=%async_computation.16 | async-start | bytes 31457280 | tf_op jit(solution)/shard_map/all_gather | solution.py:284
  11.2 2144.1 %all-gather.28.cloned.1.call-start = ((), (), s32[]{:S(2)}) async-start(), calls=%async_computation.6 | async-start | bytes 1310720 | tf_op jit(solution)/shard_map/all_gather | solution.py:324
  11.2 255.8 %collective-permute-start = (bf16[1536,2048]{1,0:T(8,128)(2,1)}, bf16[1536,2048]{1,0:T(8,128)(2,1)}, u32[]{:S(2)}, u32[]{:S(2)}) collective-permute-start(bf16[1536,2048]{1,0:T(8,128)(2,1)} %bitcast.445), channel_id=1, source_target_pairs={{0,4},{4,8},{8,12},{12,0},{1,5},{5,9},{9,13},{13,1},{2,6},{6,10},{... | collective-permute-start | bytes 18874376 | tf_op jit(solution)/shard_map/ppermute | solution.py:17
  267.1 572.3 %collective-permute-start.1 = (bf16[1536,2048]{1,0:T(8,128)(2,1)}, bf16[1536,2048]{1,0:T(8,128)(2,1)}, u32[]{:S(2)}, u32[]{:S(2)}) collective-permute-start(bf16[1536,2048]{1,0:T(8,128)(2,1)} %collective-permute-done), channel_id=1, source_target_pairs={{0,4},{4,8},{8,12},{12,0},{1,5},{5,9},{9,13},{13,1},{2,6},{6,10},{... | collective-permute-start | bytes 18874376 | tf_op jit(solution)/shard_map/ppermute | solution.py:17
  285.8 572.4 %collective-permute-start.2 = (bf16[1536,2048]{1,0:T(8,128)(2,1)}, bf16[1536,2048]{1,0:T(8,128)(2,1)}, u32[]{:S(2)}, u32[]{:S(2)}) collective-permute-start(bf16[1536,2048]{1,0:T(8,128)(2,1)} %bitcast.446), channel_id=1, source_target_pairs={{0,12},{4,0},{8,4},{12,8},{1,13},{5,1},{9,5},{13,9},{2,14},{6,2},{... | collective-permute-start | bytes 18874376 | tf_op jit(solution)/shard_map/ppermute | solution.py:19
  839.4 914.5 %copy-start.103 = (bf16[128]{0:T(256)(128)(2,1)}, bf16[128]{0:T(256)(128)(2,1)S(1)}, u32[]{:S(2)}) copy-start(bf16[128]{0:T(256)(128)(2,1)S(1)} %get-tuple-element.1149) | copy-start | bytes 772
  1750.9 3.0 collective-permute-start.3
  1800.9 158.8 %collective-permute-start.4 = (bf16[128,2048]{1,0:T(8,128)(2,1)S(1)}, bf16[128,2048]{1,0:T(8,128)(2,1)}, u32[]{:S(2)}, u32[]{:S(2)}) collective-permute-start(bf16[128,2048]{1,0:T(8,128)(2,1)S(1)} %convert_element_type.279), channel_id=1, source_target_pairs={{16,0},{17,1},{18,2},{19,3},{20,4},{21,5},{22,6},{23,7},{24,8},{25... | collective-permute-start | bytes 1572872 | tf_op jit(solution)/shard_map/ppermute | solution.py:27
  2077.7 80.7 %all-gather.26.cloned.1.call-start = ((), (), s32[]{:S(2)}) async-start(), calls=%async_computation.5 | async-start | bytes 1310720 | tf_op jit(solution)/shard_map/all_gather | solution.py:323
  2079.5 129.9 %all-gather.24.cloned.1.call-start = ((), (), s32[]{:S(2)}) async-start(), calls=%async_computation.4 | async-start | bytes 2621440 | tf_op jit(solution)/shard_map/all_gather | solution.py:322
  2081.4 175.6 %all-gather.30.cloned.1.call-start = ((), (), s32[]{:S(2)}) async-start(), calls=%async_computation.7 | async-start | bytes 2621440 | tf_op jit(solution)/shard_map/all_gather | solution.py:325
  2083.4 219.7 %all-gather.36.cloned.1.call-start = ((), (), s32[]{:S(2)}) async-start(), calls=%async_computation.10 | async-start | bytes 2621440 | tf_op jit(solution)/shard_map/all_gather | solution.py:328
  2085.4 332.7 %all-gather.34.cloned.1.call-start = ((), (), s32[]{:S(2)}) async-start(), calls=%async_computation.9 | async-start | bytes 7864320 | tf_op jit(solution)/shard_map/all_gather | solution.py:327
  2088.2 445.1 %all-gather.32.cloned.1.call-start = ((), (), s32[]{:S(2)}) async-start(), calls=%async_computation.8 | async-start | bytes 7864320 | tf_op jit(solution)/shard_map/all_gather | solution.py:326
  2092.9 17.7 all-to-all-start.2
  2110.6 21.9 all-to-all-start.1
  2132.5 16.6 all-to-all-start
  2149.1 48.0 %all-to-all-start.3 = ((bf16[128,4,1536]{0,2,1:T(8,128)(2,1)}), bf16[128,4,1536]{0,2,1:T(8,128)(2,1)S(1)}, u32[]{:S(2)}, u32[]{:S(2)}) async-start(bf16[128,4,1536]{0,2,1:T(8,128)(2,1)} %bitcast.171), calls=%async_computation.3 | async-start | bytes 3145728 | tf_op jit(solution)/shard_map/all_to_all | solution.py:319
  2153.0 830.6 %all-reduce.12.cloned.1.call-start = ((), (), s32[]{:S(2)}) async-start(), calls=%async_computation.17 | async-start | bytes 50331648 | tf_op jit(solution)/shard_map/psum | solution.py:351
  (74 other events, 6367.3 us)
Sparse Core Ops, SparseCore 0:
  9.6 150.7 all-gather.39
  161.9 125.4 all-gather.41
  289.0 337.2 all-gather.37
  627.7 200.9 all-gather.43
  830.2 424.6 all-gather.45
  1256.3 423.3 all-gather.47
  2077.8 31.9 all-gather.27
  2111.9 34.5 all-gather.25
  2148.7 60.6 all-gather.23
  2210.8 46.2 all-gather.29
  2258.6 44.4 all-gather.35
  2305.1 112.9 all-gather.33
  2420.2 112.9 all-gather.31
  2541.6 441.9 all-reduce.11
